TPU v7x, 32 devices: a whole 2x2x4 slice. The times are simulated.
32 devices in a mesh: dp: 8 (over y, x, core), mp: 4 (over z).
Axes of the slice: x: 2, y: 2, z: 4, core: 2. Of those that a mesh axis runs over, the one named last changes fastest.
Arguments:
- candidates: bfloat16 [64, 256, 768], P('dp', 'mp'), may hold values from -6 to 6
- owner_row: int32 [64], replicated, may hold values from 0 to 63, as said below
- selected: int32 [16], replicated, may hold values from 0 to 63, as said below
- dest_slot: int32 [16], replicated, may hold values from 0 to 15, as said below
- patch_weight: bfloat16 [768, 768], P(None, 'mp'), may hold values from -0.21875 to 0.21875
- positions: bfloat16 [256, 768], P(None, 'mp'), may hold values from -3 to 3
- qkv_weight: bfloat16 [768, 3, 768], P(None, None, 'mp'), may hold values from -1 to 1
- out_weight: bfloat16 [768, 768], P('mp'), may hold values from -0.21875 to 0.21875
- attn_gain: bfloat16 [768], replicated, may hold values from 0.099609375 to 1.8984375
- mlp_gain: bfloat16 [768], replicated, may hold values from 0.099609375 to 1.8984375
- up_weight: bfloat16 [768, 3072], P(None, 'mp'), may hold values from -0.21875 to 0.21875
- down_weight: bfloat16 [3072, 768], P('mp'), may hold values from -0.109375 to 0.109375
Outputs:
- layer_out: bfloat16 [16, 256, 768], P('dp', 'mp')
Inputs may be any that keep to these rules, and one draw needn't show every extreme that they name: `owner_row`: a permutation; storage row r sits on index r // 8 of dp. `selected`: distinct candidates; no index of dp stores more than 4 of them, and some index stores exactly 4. `dest_slot`: a permutation; the 2 slots s with equal s // 2 get candidates stored on different indices of dp.
All inputs are finite; a program needn't handle non-finite values.
Results may differ from a plain program's by a relative error of at most 0.012.
Values may be sent and summed in bfloat16 or wider, within the bound.
A program may use at most 128 MiB of HBM per device.

v0:
```python
import functools

import jax
import jax.numpy as jnp
from jax import lax
from jax.experimental import pallas as pl
from jax.experimental.pallas import tpu as pltpu
from jax.sharding import PartitionSpec as P

HEAD_DIM = 64
MESH = pl.DeviceIdType.MESH


def norm_rows(values, gain):
    average = jnp.mean(values, axis=-1, keepdims=True)
    centred = values - average
    variance = jnp.mean(centred * centred, axis=-1, keepdims=True)
    return centred * lax.rsqrt(variance + 1e-06) * gain


def dot(a, b):
    return jnp.dot(a, b, preferred_element_type=jnp.float32)


def dot_t(a, b):
    return lax.dot_general(a, b, (((1,), (1,)), ((), ())), preferred_element_type=jnp.float32)


def kernel(
    n_dp, n_mp, stored, per,
    owner_row, selected, dest_slot,
    cand_h, pw, pos_t, gain1, gain2, qkv_h, out_h, up_h, down_h,
    out,
    cand, qkv, out_w, up, down, pos,
    send, recv, wbuf, pbuf, xbuf, act, after, ctx, ag1, part1, ra1, rm1, rb1, ag2, part2, ra2, rm2, rb2,
    route_s, route_r, w_s, w_r, d_s, d_r, p_s, p_r, ag_s, ag_r, rs_s, rs_r, loc,
):
    dp = lax.axis_index("dp")
    mp = lax.axis_index("mp")
    quarter, width = cand.shape[1], cand.shape[2]
    feats = pw.shape[0]
    half = feats // 2
    side = mp + 1 - 2 * lax.rem(mp, 2)
    across = lax.rem(mp + n_mp // 2, n_mp)
    corner = n_mp - 1 - mp
    twin = dp + 1 - 2 * lax.rem(dp, 2)

    barrier = pltpu.get_barrier_semaphore()
    for other in (side, across, corner):
        pl.semaphore_signal(barrier, inc=1, device_id=(dp, other), device_id_type=MESH)

    @pl.loop(1, n_dp)
    def _(k):
        pl.semaphore_signal(barrier, inc=1, device_id=(lax.rem(dp + k, n_dp), mp), device_id_type=MESH)

    own_c = pltpu.make_async_copy(cand_h, cand, loc.at[5])
    own_c.start()
    own_w = pltpu.make_async_copy(pw, wbuf.at[mp], loc.at[0])
    own_w.start()
    pos[...] = jnp.transpose(pos_t[...].astype(jnp.float32)).astype(jnp.bfloat16)
    pbuf[mp] = pos[pl.ds(pl.multiple_of(mp * quarter, quarter), quarter)]
    later = [
        pltpu.make_async_copy(src, dst, loc.at[1 + j])
        for j, (src, dst) in enumerate(((qkv_h, qkv), (out_h, out_w), (up_h, up), (down_h, down)))
    ]

    pl.semaphore_wait(barrier, 3 + n_dp - 1)

    def remote(src, dst, ss, rs, where):
        return pltpu.make_async_remote_copy(
            src_ref=src, dst_ref=dst, send_sem=ss, recv_sem=rs, device_id=where, device_id_type=MESH
        )

    mine = pl.ds(pl.multiple_of(lax.rem(dp, 2) * half, half), half)
    w_side = remote(pw.at[mine], wbuf.at[mp, mine], w_s.at[0], w_r.at[0], (dp, side))
    w_across = remote(pw.at[mine], wbuf.at[mp, mine], w_s.at[1], w_r.at[1], (dp, across))
    w_across.start()
    w_side.start()
    p_copies = []
    for j, other in enumerate((side, across, corner)):
        c = remote(pos.at[pl.ds(other * quarter, quarter)], pbuf.at[mp], p_s.at[j], p_r.at[j], (dp, other))
        c.start()
        p_copies.append(c)

    count = selected.shape[0]
    short = count <= 16

    def route(i):
        row = owner_row[selected[i]]
        slot = dest_slot[i]
        owner = lax.div(row, stored)
        return slot, owner, jnp.where(owner == dp, lax.div(slot, per), -1), lax.rem(row, stored)

    routes = [route(i) for i in range(count)] if short else []

    def choose(key, value, wanted):
        if short:
            found = jnp.int32(0)
            for entry in routes:
                found = jnp.where(entry[key] == wanted, entry[value], found)
            return found

        def body(i, found):
            entry = route(i)
            return jnp.where(entry[key] == wanted, entry[value], found)
        return lax.fori_loop(0, count, body, jnp.int32(0))

    def pass_on(k):
        learner = lax.rem(dp + n_dp - k, n_dp)
        send[learner] = cand[choose(2, 3, learner)]
        remote(send.at[learner], recv.at[dp], route_s.at[learner], route_r.at[dp], (learner, mp)).start()

    own_c.wait()
    if short:
        for k in range(1, n_dp):
            pass_on(k)
    else:
        pl.loop(1, n_dp)(pass_on)
    recv[dp] = cand[choose(2, 3, dp)]
    for c in later:
        c.start()
    senders = [choose(0, 1, dp * per + e) for e in range(per)]

    w_across.wait_recv()
    w_fwd = remote(wbuf.at[across, mine], wbuf.at[across, mine], w_s.at[2], w_r.at[2], (dp, side))
    w_fwd.start()
    d_copies = []

    def to_twin(j, block):
        c = remote(wbuf.at[block, mine], wbuf.at[block, mine], d_s.at[j], d_r.at[j], (twin, mp))
        c.start()
        d_copies.append(c)

    to_twin(0, across)
    w_side.wait_recv()
    to_twin(1, side)
    for c in p_copies:
        c.wait()
    for g in range(n_mp):
        act[:, g * feats:(g + 1) * feats] = jnp.concatenate([pbuf[g].astype(jnp.float32)] * per, axis=0)
    w_fwd.wait_recv()
    to_twin(2, corner)

    @pl.loop(1, n_dp)
    def _(k):
        peer = lax.rem(dp + k, n_dp)
        remote(send.at[peer], recv.at[peer], route_s.at[peer], route_r.at[peer], (peer, mp)).wait()

    own_w.wait()
    for e in range(per):
        xbuf[e * quarter:(e + 1) * quarter] = recv[senders[e]]
    for c in d_copies:
        c.wait()
    for c in (w_side, w_across, w_fwd):
        c.wait_send()

    prod = dot_t(xbuf[...], wbuf[...].reshape(n_mp * feats, width))
    act[...] = (prod + act[...]).astype(jnp.bfloat16).astype(jnp.float32)

    def gather_start(buf, base, e):
        cs = []
        for j, other in enumerate((across, side)):
            c = remote(buf.at[e, mp], buf.at[e, mp], ag_s.at[base + j], ag_r.at[base + j], (dp, other))
            c.start()
            cs.append(c)
        return cs

    def gather_forward(buf, base, e, cs):
        cs[0].wait_recv()
        c = remote(buf.at[e, across], buf.at[e, across], ag_s.at[base + 2], ag_r.at[base + 2], (dp, side))
        c.start()
        cs.append(c)

    def gather_end(cs):
        cs[1].wait_recv()
        cs[2].wait_recv()
        for c in cs:
            c.wait_send()

    def sum_start(part, ra, base, e):
        cs = []
        for j, block in enumerate((corner, side)):
            c = remote(part.at[e, block], ra.at[e, j], rs_s.at[base + j], rs_r.at[base + j], (dp, side))
            c.start()
            cs.append(c)
        return cs

    def sum_merge(part, ra, rm, rb, base, e, cs):
        cs[0].wait_recv()
        rm[e] = (part[e, across].astype(jnp.float32) + ra[e, 0].astype(jnp.float32)).astype(jnp.bfloat16)
        c = remote(rm.at[e], rb.at[e], rs_s.at[base + 2], rs_r.at[base + 2], (dp, across))
        c.start()
        cs.append(c)

    def sum_end(part, ra, rb, e, cs):
        cs[1].wait_recv()
        cs[2].wait_recv()
        for c in cs:
            c.wait_send()
        return part[e, mp].astype(jnp.float32) + ra[e, 1].astype(jnp.float32) + rb[e].astype(jnp.float32)

    def rows(e):
        return pl.ds(e * quarter, quarter)

    g1 = gain1[...].astype(jnp.float32).reshape(1, width)
    g2 = gain2[...].astype(jnp.float32).reshape(1, width)
    every = range(per)
    gathers = []
    for e in every:
        ag1[e, mp] = norm_rows(act[rows(e)], g1).astype(jnp.bfloat16)
        gathers.append(gather_start(ag1, 3 * e, e))
    for e in every:
        gather_forward(ag1, 3 * e, e, gathers[e])

    tokens = n_mp * quarter
    sums = []
    for e in every:
        gather_end(gathers[e])
        if e == 0:
            later[0].wait()
            later[1].wait()
        normed = ag1[e].reshape(tokens, width)
        qkv_all = dot_t(normed, qkv[...].reshape(3 * feats, width)).astype(jnp.bfloat16)
        q = qkv_all[:, :feats] * jnp.bfloat16(HEAD_DIM ** (-0.5))
        k = qkv_all[:, feats:2 * feats]
        v = qkv_all[:, 2 * feats:]
        for h in range(feats // HEAD_DIM):
            cut = slice(h * HEAD_DIM, (h + 1) * HEAD_DIM)
            s = dot_t(q[:, cut], k[:, cut])
            p = jnp.exp(s - jnp.max(s, axis=-1, keepdims=True))
            total = jnp.sum(p, axis=-1, keepdims=True)
            ctx[:, cut] = (dot(p.astype(jnp.bfloat16), v[:, cut]) / total).astype(jnp.bfloat16)
        part1[e] = dot(ctx[...], out_w[...]).astype(jnp.bfloat16).reshape(n_mp, quarter, width)
        sums.append(sum_start(part1, ra1, 3 * e, e))
    for e in every:
        sum_merge(part1, ra1, rm1, rb1, 3 * e, e, sums[e])
    gathers = []
    for e in every:
        value = act[rows(e)] + sum_end(part1, ra1, rb1, e, sums[e])
        after[rows(e)] = value
        ag2[e, mp] = norm_rows(value, g2).astype(jnp.bfloat16)
        gathers.append(gather_start(ag2, 3 * (per + e), e))
    for e in every:
        gather_forward(ag2, 3 * (per + e), e, gathers[e])
    sums = []
    for e in every:
        gather_end(gathers[e])
        if e == 0:
            later[2].wait()
            later[3].wait()
        x = dot(ag2[e].reshape(tokens, width), up[...])
        hidden = (0.5 * x * (1.0 + lax.erf(x * 0.7071067811865476))).astype(jnp.bfloat16)
        part2[e] = dot(hidden, down[...]).astype(jnp.bfloat16).reshape(n_mp, quarter, width)
        sums.append(sum_start(part2, ra2, 3 * (per + e), e))
    for e in every:
        sum_merge(part2, ra2, rm2, rb2, 3 * (per + e), e, sums[e])
    for e in every:
        out[e] = (after[rows(e)] + sum_end(part2, ra2, rb2, e, sums[e])).astype(jnp.bfloat16)


def solution(mesh):
    n_dp, n_mp = mesh.shape["dp"], mesh.shape["mp"]

    def local(
        candidates, owner_row, selected, dest_slot, patch_weight, positions,
        qkv_weight, out_weight, attn_gain, mlp_gain, up_weight, down_weight,
    ):
        stored, quarter, width = candidates.shape
        per = selected.shape[0] // n_dp
        feats = patch_weight.shape[1]
        qkv = jnp.transpose(qkv_weight, (1, 2, 0))
        vm = pl.BlockSpec(memory_space=pltpu.VMEM)
        hb = pl.BlockSpec(memory_space=pl.ANY)
        sm = pl.BlockSpec(memory_space=pltpu.SMEM)
        bf, f32 = jnp.bfloat16, jnp.float32
        blocks = pltpu.VMEM((per, n_mp, quarter, width), bf)
        pair = pltpu.VMEM((per, 2, quarter, width), bf)
        one = pltpu.VMEM((per, quarter, width), bf)
        dma = pltpu.SemaphoreType.DMA
        return pl.pallas_call(
            functools.partial(kernel, n_dp, n_mp, stored, per),
            out_shape=jax.ShapeDtypeStruct((per, quarter, width), bf),
            in_specs=[sm] * 3 + [hb] * 2 + [vm] * 3 + [hb] * 4,
            out_specs=vm,
            scratch_shapes=[
                pltpu.VMEM(candidates.shape, bf), pltpu.VMEM(qkv.shape, bf), pltpu.VMEM(out_weight.shape, bf),
                pltpu.VMEM(up_weight.shape, bf), pltpu.VMEM(down_weight.shape, bf),
                pltpu.VMEM(positions.shape, bf),
                pltpu.VMEM((n_dp, quarter, width), bf),
                pltpu.VMEM((n_dp, quarter, width), bf),
                pltpu.VMEM((n_mp, feats, width), bf),
                pltpu.VMEM((n_mp, quarter, feats), bf),
                pltpu.VMEM((per * quarter, width), bf),
                pltpu.VMEM((per * quarter, n_mp * feats), f32),
                pltpu.VMEM((per * quarter, n_mp * feats), f32),
                pltpu.VMEM((n_mp * quarter, feats), bf),
                blocks, blocks, pair, one, one,
                blocks, blocks, pair, one, one,
                dma((n_dp,)), dma((n_dp,)),
                dma((3,)), dma((3,)), dma((3,)), dma((3,)), dma((3,)), dma((3,)),
                dma((6 * per,)), dma((6 * per,)), dma((6 * per,)), dma((6 * per,)),
                dma((6,)),
            ],
            compiler_params=pltpu.CompilerParams(
                collective_id=0, has_side_effects=True, vmem_limit_bytes=60000 * 1024
            ),
        )(
            owner_row, selected, dest_slot, candidates, patch_weight.T, positions.T,
            attn_gain, mlp_gain, qkv, out_weight, up_weight, down_weight,
        )

    return jax.shard_map(
        local,
        mesh=mesh,
        in_specs=(
            P("dp", "mp", None), P(), P(), P(), P(None, "mp"), P(None, "mp"), P(None, None, "mp"),
            P("mp", None), P(), P(), P(None, "mp"), P("mp", None),
        ),
        out_specs=P("dp", "mp", None),
        check_vma=False,
    )
```

profile of v0, /device:TPU:0, one launch (start us, length us, event | category | flops | bytes accessed | tf_op | source)
XLA Modules:
  0.0 82.1 jit_solution(16895311657300945443)
XLA Ops:
  0.0 80.5 %shard_map.118 = bf16[2,64,768]{2,1,0:T(8,128)(2,1)} custom-call(s32[64]{0:T(128)} %owner_row.1, s32[16]{0:T(128)} %selected.1, s32[16]{0:T(128)} %dest_slot.1, bf16[8,64,768]{2,1,0:T(8,128)(2,1)} %cand_h.1, bf16[192,768]{1,0:T(8,128)(2,1)} %bitcast.4, bf16[192,256]{1,0:T(8,128)(2,1)} %bitcast.5, bf16[768]{0:T(1024)(128)(2,1)} %gain1.1, ...), custom_call_target="tpu_custom_call" | custom-call | tf_op jit(solution)/shard_map/pallas_call | solution.py:280
  80.5 1.6 %copy.14 = bf16[2,64,768]{2,1,0:T(8,128)(2,1)} copy(bf16[2,64,768]{2,1,0:T(8,128)(2,1)} %shard_map.118) | data formatting | bytes 393216
where the time goes:
time: 82.3 us; the launch traced here: 82.1 us
  Pallas kernels  80.5 us (98%)
  local copies, waits for them, and re-layouts  1.62 us (2%)
    pallas_call x1, Pallas kernels, local(): pl.pallas_call(functools.partial(kernel, n_dp, n_mp, stored, per), out_sh...  80.5 us

commit v1 on v0

v1 whole, which is shorter than its diff:
```python
import functools

import jax
import jax.numpy as jnp
from jax import lax
from jax.experimental import pallas as pl
from jax.experimental.pallas import tpu as pltpu
from jax.sharding import PartitionSpec as P

HEAD_DIM = 64
LANES = 128
PARTS = 2
MESH = pl.DeviceIdType.MESH
scope = jax.named_scope


def norm_rows(values, gain):
    average = jnp.mean(values, axis=-1, keepdims=True)
    centred = values - average
    variance = jnp.mean(centred * centred, axis=-1, keepdims=True)
    return centred * lax.rsqrt(variance + 1e-06) * gain


def dot(a, b):
    return jnp.dot(a, b, preferred_element_type=jnp.float32)


def dot_t(a, b):
    return lax.dot_general(a, b, (((1,), (1,)), ((), ())), preferred_element_type=jnp.float32)


def kernel(
    n_dp, n_mp, stored, per,
    owner_row, selected, dest_slot,
    cand_h, pw, pos_t, gain1, gain2, qkv_h, out_h, up_h, down_h,
    out_hbm,
    cand, qkv, up, down, wrel, orel, posf,
    send, recv0, recv1, xr, n1, act, after, ctx, cx, n2, part, ra, rm, rb, out,
    route_s, route_r, wz_s, wz_r, wx_s, wx_r, wt_s, wt_r, oz_s, oz_r, ox_s, ox_r, ot_s, ot_r,
    ag_s, ag_r, cx_s, cx_r, rs_s, rs_r, loc,
):
    dp = lax.axis_index("dp")
    mp = lax.axis_index("mp")
    recvs = (recv0, recv1)
    quarter, width = cand.shape[1], cand.shape[2]
    feats = pw.shape[0]
    rows = quarter // PARTS
    tokens = n_mp * quarter
    group = wrel.shape[2] // LANES
    side = mp + 1 - 2 * lax.rem(mp, 2)
    across = lax.rem(mp + n_mp // 2, n_mp)
    corner = n_mp - 1 - mp
    rel = (mp, side, across, corner)
    twin = dp + 1 - 2 * lax.rem(dp, 2)
    place = lax.rem(dp, group)
    first = dp - place
    mates = group // 2 - 1

    barrier = pltpu.get_barrier_semaphore()
    for other in rel[1:]:
        pl.semaphore_signal(barrier, inc=1, device_id=(dp, other), device_id_type=MESH)

    @pl.loop(1, n_dp)
    def _(k):
        pl.semaphore_signal(barrier, inc=1, device_id=(lax.rem(dp + k, n_dp), mp), device_id_type=MESH)

    own_w = pltpu.make_async_copy(pw, wrel.at[0, :, pl.ds(0, width)], loc.at[0])
    own_p = pltpu.make_async_copy(pos_t, wrel.at[0, :, pl.ds(width, tokens)], loc.at[1])
    own_o = pltpu.make_async_copy(out_h, orel.at[0], loc.at[2])
    own_c = pltpu.make_async_copy(cand_h, cand, loc.at[3])
    for c in (own_w, own_p, own_c, own_o):
        c.start()
    later = [
        pltpu.make_async_copy(src, dst, loc.at[4 + j])
        for j, (src, dst) in enumerate(((qkv_h, qkv), (up_h, up), (down_h, down)))
    ]
    count = selected.shape[0]
    short = count <= 16

    def route(i):
        row = owner_row[selected[i]]
        slot = dest_slot[i]
        owner = lax.div(row, stored)
        return slot, owner, jnp.where(owner == dp, lax.div(slot, per), -1), lax.rem(row, stored)

    routes = [route(i) for i in range(count)] if short else []

    def choose(key, value, wanted):
        if short:
            found = jnp.int32(0)
            for entry in routes:
                found = jnp.where(entry[key] == wanted, entry[value], found)
            return found

        def body(i, found):
            entry = route(i)
            return jnp.where(entry[key] == wanted, entry[value], found)
        return lax.fori_loop(0, count, body, jnp.int32(0))

    def remote(src, dst, ss, rs, where):
        return pltpu.make_async_remote_copy(
            src_ref=src, dst_ref=dst, send_sem=ss, recv_sem=rs, device_id=where, device_id_type=MESH
        )

    def w_cut(j):
        return pl.ds(0, feats), pl.ds(pl.multiple_of(j * LANES, LANES), LANES)

    o_rows, o_cols = 2 * feats // group, width // 2

    def o_cut(j):
        return (
            pl.ds(pl.multiple_of(lax.div(j, 2) * o_rows, o_rows), o_rows),
            pl.ds(pl.multiple_of(lax.rem(j, 2) * o_cols, o_cols), o_cols),
        )

    unsent = []

    def go(c):
        c.start()
        unsent.append(c)
        return c

    class Spread:
        def __init__(self, buf, cut, zs, zr, xs, xr_, ts, tr):
            self.buf, self.cut = buf, cut
            self.zs, self.zr, self.xs, self.xr, self.ts, self.tr = zs, zr, xs, xr_, ts, tr

        def over_z(self):
            cut = self.cut(place)
            self.z = [
                go(remote(self.buf.at[(0, *cut)], self.buf.at[(r, *cut)], self.zs.at[r - 1], self.zr.at[r - 1], (dp, rel[r])))
                for r in (2, 3, 1)
            ]

        def block(self, j):
            return self.buf.at[(pl.ds(1, n_mp - 1), *self.cut(j))]

        def over_xy(self):
            for c in self.z:
                c.wait_recv()
            mine = self.block(place)
            self.x = []
            for k in range(1, mates + 1):
                peer = first + lax.rem(place + 2 * k, group)
                self.x.append(go(remote(mine, mine, self.xs.at[k - 1], self.xr.at[k - 1], (peer, mp))))
            self.t = [go(remote(mine, mine, self.ts.at[0], self.tr.at[0], (twin, mp)))]

        def to_twin(self, k):
            self.x[k - 1].wait_recv()
            got = self.block(lax.rem(place + group - 2 * k, group))
            self.t.append(go(remote(got, got, self.ts.at[k], self.tr.at[k], (twin, mp))))

        def end(self):
            for c in self.t:
                c.wait_recv()

    spread_w = Spread(wrel, w_cut, wz_s, wz_r, wx_s, wx_r, wt_s, wt_r)
    spread_o = Spread(orel, o_cut, oz_s, oz_r, ox_s, ox_r, ot_s, ot_r)

    for c in (own_w, own_p, own_c, own_o):
        c.wait()
    with scope("s_barrier"):
        pl.semaphore_wait(barrier, n_mp - 1 + n_dp - 1)

    with scope("s_pass"):
        spread_w.over_z()
        for h in range(PARTS):
            def pass_on(k):
                learner = lax.rem(dp + n_dp - k, n_dp)
                send[h, learner] = cand[choose(2, 3, learner), h * rows:(h + 1) * rows]
                remote(
                    send.at[h, learner], recvs[h].at[dp], route_s.at[h, learner], route_r.at[h, dp], (learner, mp)
                ).start()

            if short:
                for k in range(1, n_dp):
                    pass_on(k)
            else:
                pl.loop(1, n_dp)(pass_on)
            recvs[h][dp] = cand[choose(2, 3, dp), h * rows:(h + 1) * rows]
        spread_o.over_z()
        for c in later:
            c.start()
        senders = [choose(0, 1, dp * per + e) for e in range(per)]

    def gather_start(buf, base, e, h):
        at = 3 * (base + e * PARTS + h)
        return [
            go(remote(buf.at[e, h, 0], buf.at[e, h, r], ag_s.at[at + j], ag_r.at[at + j], (dp, rel[r])))
            for j, r in enumerate((2, 1))
        ]

    def gather_forward(buf, base, e, h, cs):
        at = 3 * (base + e * PARTS + h) + 2
        cs[0].wait_recv()
        cs.append(go(remote(buf.at[e, h, 2], buf.at[e, h, 3], ag_s.at[at], ag_r.at[at], (dp, side))))

    def gather_end(cs):
        cs[1].wait_recv()
        cs[2].wait_recv()

    every = range(per)
    halves = range(PARTS)
    gathers = {}
    with scope("s_wxy"):
        spread_w.over_xy()
    for h in halves:
        with scope("s_route"):
            @pl.loop(1, n_dp)
            def _(k):
                peer = lax.rem(dp + k, n_dp)
                remote(
                    send.at[h, peer], recvs[h].at[peer], route_s.at[h, peer], route_r.at[h, peer], (peer, mp)
                ).wait()

            for e in every:
                xr[e, h, 0] = recvs[h][senders[e]]
                gathers[e, h] = gather_start(xr, 0, e, h)
        if h == 0:
            with scope("s_oxy"):
                spread_o.over_xy()
    with scope("s_fwd1a"):
        for e in every:
            gather_forward(xr, 0, e, 0, gathers[e, 0])
    with scope("s_wtwin"):
        for k in range(1, mates + 1):
            spread_w.to_twin(k)
    with scope("s_fwd1b"):
        gather_forward(xr, 0, 0, 1, gathers[0, 1])
    with scope("s_wend"):
        spread_w.end()
    with scope("s_pos"):
        for q in range(n_mp):
            posf[:, q * feats:(q + 1) * feats] = jnp.transpose(wrel[rel[q], :, width:].astype(jnp.float32))

    g1 = gain1[...].astype(jnp.float32).reshape(1, width)
    g2 = gain2[...].astype(jnp.float32).reshape(1, width)

    def embed(e, h):
        w = jnp.concatenate([wrel[rel[q], :, :width] for q in range(n_mp)], axis=0)
        pos = jnp.concatenate(
            [posf[pl.ds(pl.multiple_of(rel[r] * quarter + h * rows, rows), rows)] for r in range(n_mp)], axis=0
        )
        prod = dot_t(xr[e, h].reshape(n_mp * rows, width), w)
        value = (prod + pos).astype(jnp.bfloat16).astype(jnp.float32)
        act[e, h] = value[:rows]
        n1[e, h * n_mp * rows:(h + 1) * n_mp * rows] = norm_rows(value, g1).astype(jnp.bfloat16)

    def attend(e):
        qkv_all = dot_t(n1[e], qkv[...].reshape(3 * feats, width)).astype(jnp.bfloat16)
        q = qkv_all[:, :feats] * jnp.bfloat16(HEAD_DIM ** (-0.5))
        k = qkv_all[:, feats:2 * feats]
        v = qkv_all[:, 2 * feats:]
        for head in range(feats // HEAD_DIM):
            cut = slice(head * HEAD_DIM, (head + 1) * HEAD_DIM)
            s = dot_t(q[:, cut], k[:, cut])
            p = jnp.exp(s - jnp.max(s, axis=-1, keepdims=True))
            total = jnp.sum(p, axis=-1, keepdims=True)
            c = (dot(p.astype(jnp.bfloat16), v[:, cut]) / total).astype(jnp.bfloat16)
            ctx[e, :, :, :, cut] = c.reshape(PARTS, n_mp, rows, HEAD_DIM)
        return [
            go(remote(ctx.at[e, :, r], cx.at[e, r - 1], cx_s.at[3 * e + r - 1], cx_r.at[3 * e + r - 1], (dp, rel[r])))
            for r in (3, 2, 1)
        ]

    def project(e, cs):
        for c in cs:
            c.wait_recv()
        total = dot(ctx[e, :, 0].reshape(quarter, feats), orel[0])
        for r in range(1, n_mp):
            total += dot(cx[e, r - 1].reshape(quarter, feats), orel[r])
        value = act[e].reshape(quarter, width) + total
        after[e] = value.reshape(PARTS, rows, width)
        normed = norm_rows(value, g2).astype(jnp.bfloat16)
        for h in halves:
            n2[e, h, 0] = normed[h * rows:(h + 1) * rows]
            gathers[e, h] = gather_start(n2, per * PARTS, e, h)

    sums = {}

    def mlp(e, h):
        x = dot(n2[e, h].reshape(n_mp * rows, width), up[...])
        hidden = (0.5 * x * (1.0 + lax.erf(x * 0.7071067811865476))).astype(jnp.bfloat16)
        part[e, h] = dot(hidden, down[...]).astype(jnp.bfloat16).reshape(n_mp, rows, width)
        at = 3 * (e * PARTS + h)
        sums[e, h] = [
            go(remote(part.at[e, h, r], ra.at[e, h, j], rs_s.at[at + j], rs_r.at[at + j], (dp, side)))
            for j, r in enumerate((3, 1))
        ]

    def merge(e, h):
        at = 3 * (e * PARTS + h) + 2
        sums[e, h][0].wait_recv()
        rm[e, h] = (part[e, h, 2].astype(jnp.float32) + ra[e, h, 0].astype(jnp.float32)).astype(jnp.bfloat16)
        sums[e, h].append(go(remote(rm.at[e, h], rb.at[e, h], rs_s.at[at], rs_r.at[at], (dp, across))))

    def finish(e, h):
        cs = sums[e, h]
        cs[1].wait_recv()
        cs[2].wait_recv()
        total = part[e, h, 0].astype(jnp.float32) + ra[e, h, 1].astype(jnp.float32) + rb[e, h].astype(jnp.float32)
        out[e, h] = (after[e, h] + total).astype(jnp.bfloat16)
        c = pltpu.make_async_copy(out.at[e, h], out_hbm.at[e, pl.ds(h * rows, rows)], loc.at[7 + e * PARTS + h])
        c.start()
        return c

    contexts = []
    for e in every:
        for h in halves:
            if (e, h) == (per - 1, PARTS - 1):
                with scope("s_fwd1c"):
                    gather_forward(xr, 0, e, h, gathers[e, h])
            with scope("s_ag1end"):
                gather_end(gathers[e, h])
            with scope("s_embed"):
                embed(e, h)
        if e == 0:
            with scope("s_otwin"):
                for k in range(1, mates + 1):
                    spread_o.to_twin(k)
                later[0].wait()
        else:
            with scope("s_proj0"):
                spread_o.end()
                project(e - 1, contexts[e - 1])
        with scope("s_attend"):
            contexts.append(attend(e))
    with scope("s_fwd2a"):
        for h in halves:
            gather_forward(n2, per * PARTS, 0, h, gathers[0, h])
    with scope("s_proj1"):
        project(per - 1, contexts[per - 1])
    for c in later[1:]:
        c.wait()
    for h in halves:
        with scope("s_ag2a"):
            gather_end(gathers[0, h])
        with scope("s_mlp"):
            mlp(0, h)
    for h in halves:
        with scope("s_fwd2b"):
            gather_forward(n2, per * PARTS, 1, h, gathers[1, h])
        with scope("s_merge0"):
            merge(0, h)
    for h in halves:
        with scope("s_ag2b"):
            gather_end(gathers[1, h])
        with scope("s_mlp"):
            mlp(1, h)
    outs = []
    with scope("s_fin0"):
        for h in halves:
            outs.append(finish(0, h))
    for h in halves:
        with scope("s_merge1"):
            merge(1, h)
    for h in halves:
        with scope("s_fin1"):
            outs.append(finish(1, h))
    with scope("s_drain"):
        for c in unsent:
            c.wait_send()
        for c in outs:
            c.wait()


def solution(mesh):
    n_dp, n_mp = mesh.shape["dp"], mesh.shape["mp"]

    def local(
        candidates, owner_row, selected, dest_slot, patch_weight, positions,
        qkv_weight, out_weight, attn_gain, mlp_gain, up_weight, down_weight,
    ):
        stored, quarter, width = candidates.shape
        per = selected.shape[0] // n_dp
        feats = patch_weight.shape[1]
        tokens = positions.shape[0]
        rows = quarter // PARTS
        group = (width + tokens) // LANES
        mates = group // 2 - 1
        qkv = jnp.transpose(qkv_weight, (1, 2, 0))
        vm = pl.BlockSpec(memory_space=pltpu.VMEM)
        hb = pl.BlockSpec(memory_space=pl.ANY)
        sm = pl.BlockSpec(memory_space=pltpu.SMEM)
        bf, f32 = jnp.bfloat16, jnp.float32
        dma = pltpu.SemaphoreType.DMA
        chunks = per * PARTS
        return pl.pallas_call(
            functools.partial(kernel, n_dp, n_mp, stored, per),
            out_shape=jax.ShapeDtypeStruct((per, quarter, width), bf),
            in_specs=[sm] * 3 + [hb] * 3 + [vm] * 2 + [hb] * 4,
            out_specs=hb,
            scratch_shapes=[
                pltpu.VMEM(candidates.shape, bf), pltpu.VMEM(qkv.shape, bf),
                pltpu.VMEM(up_weight.shape, bf), pltpu.VMEM(down_weight.shape, bf),
                pltpu.VMEM((n_mp, feats, width + tokens), bf),
                pltpu.VMEM((n_mp, feats, width), bf),
                pltpu.VMEM((tokens, width), f32),
                pltpu.VMEM((PARTS, n_dp, rows, width), bf),
                pltpu.VMEM((n_dp, rows, width), bf), pltpu.VMEM((n_dp, rows, width), bf),
                pltpu.VMEM((per, PARTS, n_mp, rows, width), bf),
                pltpu.VMEM((per, tokens, width), bf),
                pltpu.VMEM((per, PARTS, rows, width), f32),
                pltpu.VMEM((per, PARTS, rows, width), f32),
                pltpu.VMEM((per, PARTS, n_mp, rows, feats), bf),
                pltpu.VMEM((per, n_mp - 1, PARTS, rows, feats), bf),
                pltpu.VMEM((per, PARTS, n_mp, rows, width), bf),
                pltpu.VMEM((per, PARTS, n_mp, rows, width), bf),
                pltpu.VMEM((per, PARTS, 2, rows, width), bf),
                pltpu.VMEM((per, PARTS, rows, width), bf),
                pltpu.VMEM((per, PARTS, rows, width), bf),
                pltpu.VMEM((per, PARTS, rows, width), bf),
                dma((PARTS, n_dp)), dma((PARTS, n_dp)),
                dma((3,)), dma((3,)), dma((mates,)), dma((mates,)), dma((mates + 1,)), dma((mates + 1,)),
                dma((3,)), dma((3,)), dma((mates,)), dma((mates,)), dma((mates + 1,)), dma((mates + 1,)),
                dma((6 * chunks,)), dma((6 * chunks,)),
                dma((3 * per,)), dma((3 * per,)),
                dma((3 * chunks,)), dma((3 * chunks,)),
                dma((7 + chunks,)),
            ],
            compiler_params=pltpu.CompilerParams(
                collective_id=0, has_side_effects=True, vmem_limit_bytes=60 * 1024 * 1024
            ),
        )(
            owner_row, selected, dest_slot, candidates, patch_weight.T, positions.T,
            attn_gain, mlp_gain, qkv, out_weight, up_weight, down_weight,
        )

    return jax.shard_map(
        local,
        mesh=mesh,
        in_specs=(
            P("dp", "mp", None), P(), P(), P(), P(None, "mp"), P(None, "mp"), P(None, None, "mp"),
            P("mp", None), P(), P(), P(None, "mp"), P("mp", None),
        ),
        out_specs=P("dp", "mp", None),
        check_vma=False,
    )
```

time: 82.3 us -> 71 us (0.86)
  Pallas kernels: 80.5 us -> 69.2 us
    pallas_call x1, Pallas kernels: 80.5 us -> 69.2 us  [local(): pl.pallas_call(functools.partial(kernel, n_dp, n_mp, stored, per), out_sh...]
where the time goes in v1:
time: 71 us; the launch traced here: 70.8 us
  Pallas kernels  69.2 us (97%)
  local copies, waits for them, and re-layouts  1.62 us (2%)
    pallas_call x1, Pallas kernels, local(): pl.pallas_call(functools.partial(kernel, n_dp, n_mp, stored, per), out_sh...  69.2 us
    unnamed x1, local copies, waits for them, and re-layouts  1.62 us

profile of v1, /device:TPU:0, one launch (start us, length us, event | category | flops | bytes accessed | tf_op | source)
XLA Modules:
  0.0 70.8 jit_solution(1326651141867549101)
XLA Ops:
  0.0 69.2 %shard_map.118 = bf16[2,64,768]{2,1,0:T(8,128)(2,1)} custom-call(s32[64]{0:T(128)} %owner_row.1, s32[16]{0:T(128)} %selected.1, s32[16]{0:T(128)} %dest_slot.1, bf16[8,64,768]{2,1,0:T(8,128)(2,1)} %cand_h.1, bf16[192,768]{1,0:T(8,128)(2,1)} %bitcast.4, bf16[192,256]{1,0:T(8,128)(2,1)} %bitcast.5, bf16[768]{0:T(1024)(128)(2,1)} %gain1.1, ...), custom_call_target="tpu_custom_call" | custom-call | tf_op jit(solution)/shard_map/pallas_call | solution.py:388
  69.2 1.6 %copy.14 = bf16[2,64,768]{2,1,0:T(8,128)(2,1)} copy(bf16[2,64,768]{2,1,0:T(8,128)(2,1)} %shard_map.118) | data formatting | bytes 393216
